TPU v7x, 32 devices: a whole 2x2x4 slice. The times are simulated.
32 devices in a mesh: groups: 2 (over y), blk: 4 (over z), sub: 4 (over x, core).
Axes of the slice: x: 2, y: 2, z: 4, core: 2. Of those that a mesh axis runs over, the one named last changes fastest.
Arguments:
- dense_coef: float32 [256, 128, 128], P(('groups', 'blk'), 'sub'), parts along dimension 0, may hold values from -6 to 6
- sparse_coef: float32 [8, 128, 128], P(('groups', 'blk'), 'sub'), parts along dimension 0, may hold values from -0.0234375 to 0.0234375
- pattern: int32 [8], P('groups'), parts along dimension 0, may hold values from 0 to 159, as said below
Outputs:
- product_coef: float32 [256, 128, 128], P(('groups', 'blk'), 'sub'), parts along dimension 0
There are 2 independent parts, one for each index of `groups`. A program takes and returns all parts, laid end to end along the dimension named above; each array names one. Nothing has to cross between parts.
Inputs may be any that keep to these rules, and one draw needn't show every extreme that they name: `pattern`: the 4 entries are distinct.
All inputs are finite; a program needn't handle non-finite values.
Results may differ from a plain program's by a relative error of at most 0.000076.
Values sent between devices are 32-bit elements; how exact they have to be, the bound alone decides.
No kernel may reach another device: no remote copies, remote signals or barrier semaphores. Data moves between devices by JAX's collectives and lax.ppermute only.
A program may use at most 128 MiB of HBM per device.

v0:
```python
import math
import jax
import jax.numpy as jnp
from jax import lax
from jax.sharding import PartitionSpec as P

STEPS = 5
exact_setting = lax.Precision.HIGHEST


def shifted(block, axis, distance):
    devices = range(lax.axis_size(axis))
    route = [((i - distance) % len(devices), i) for i in devices]
    return lax.ppermute(block, axis, route)


def angle_table(row_total, col_total, period, row_start, col_start):
    row_ids = jnp.arange(row_total, dtype=jnp.int32)[:, None] + row_start
    col_ids = jnp.arange(col_total, dtype=jnp.int32)[None, :] + col_start
    phases = jnp.mod(row_ids * col_ids, period).astype(jnp.float32) * (2.0 * math.pi / period)
    return (jnp.cos(phases), jnp.sin(phases))


def forward(series_coefficients):
    col_local = series_coefficients.shape[1]
    row_total = series_coefficients.shape[2]
    padded = 2 * row_total
    col_total = col_local * lax.axis_size("sub")
    period = padded * col_total
    cosine_lookup, sine_lookup = angle_table(row_total, padded, padded, 0, 0)
    initial_real = jnp.einsum(
        "ufz,ze->ufe", series_coefficients, cosine_lookup, precision=exact_setting
    )
    initial_imaginary = -jnp.einsum(
        "ufz,ze->ufe", series_coefficients, sine_lookup, precision=exact_setting
    )
    twist_cos, twist_sin = angle_table(
        col_local, padded, period, lax.axis_index("sub") * col_local, 0
    )
    turned_real = initial_real * twist_cos + initial_imaginary * twist_sin
    turned_imag = initial_imaginary * twist_cos - initial_real * twist_sin
    stacked = jnp.stack([turned_real, turned_imag], axis=0)
    outer_cosine, outer_sine = angle_table(col_total, col_total, col_total, 0, 0)
    halves = lax.all_to_all(stacked, "sub", split_axis=3, concat_axis=2, tiled=True)
    partial_real = halves[0]
    partial_imaginary = halves[1]
    output_real = jnp.einsum(
        "rxs,xl->rsl", partial_real, outer_cosine, precision=exact_setting
    ) + jnp.einsum("rxs,xl->rsl", partial_imaginary, outer_sine, precision=exact_setting)
    output_imaginary = jnp.einsum(
        "rxs,xl->rsl", partial_imaginary, outer_cosine, precision=exact_setting
    ) - jnp.einsum("rxs,xl->rsl", partial_real, outer_sine, precision=exact_setting)
    return jnp.stack([output_real, output_imaginary], axis=0)


def flatten(halves):
    return (halves[0].reshape(halves[0].shape[0], -1), halves[1].reshape(halves[1].shape[0], -1))


def accumulate(totals, source, sparse, pattern, start):
    source_len = source[0].shape[0]
    targets = jnp.arange(totals[0].shape[0], dtype=jnp.int32)

    def one_entry(entry, running):
        wanted = start + targets - pattern[entry]
        valid = jnp.logical_and(wanted >= 0, wanted < source_len)[:, None]
        safe = jnp.clip(wanted, 0, source_len - 1)
        src_real = jnp.where(valid, jnp.take(source[0], safe, axis=0), 0.0)
        src_imag = jnp.where(valid, jnp.take(source[1], safe, axis=0), 0.0)
        sp_real = sparse[0][entry][None, :]
        sp_imag = sparse[1][entry][None, :]
        return (
            running[0] + src_real * sp_real - src_imag * sp_imag,
            running[1] + src_real * sp_imag + src_imag * sp_real,
        )

    return lax.fori_loop(0, pattern.shape[0], one_entry, totals)


def inverse(totals, local_rows, col_total):
    block_count = totals[0].shape[0]
    spectrum_real = totals[0].reshape(block_count, local_rows, col_total)
    spectrum_imaginary = totals[1].reshape(block_count, local_rows, col_total)
    padded = local_rows * lax.axis_size("sub")
    period = padded * col_total
    outer_cosine, outer_sine = angle_table(col_total, col_total, col_total, 0, 0)
    combined_real = jnp.einsum(
        "ahz,zr->arh", spectrum_real, outer_cosine, precision=exact_setting
    ) - jnp.einsum("ahz,zr->arh", spectrum_imaginary, outer_sine, precision=exact_setting)
    combined_imaginary = jnp.einsum(
        "ahz,zr->arh", spectrum_real, outer_sine, precision=exact_setting
    ) + jnp.einsum("ahz,zr->arh", spectrum_imaginary, outer_cosine, precision=exact_setting)
    twist_cos, twist_sin = angle_table(
        col_total, local_rows, period, 0, lax.axis_index("sub") * local_rows
    )
    turned_real = combined_real * twist_cos - combined_imaginary * twist_sin
    turned_imag = combined_real * twist_sin + combined_imaginary * twist_cos
    inverse_step_real, inverse_step_imaginary = (
        lax.all_to_all(turned_real, "sub", split_axis=1, concat_axis=2, tiled=True),
        lax.all_to_all(turned_imag, "sub", split_axis=1, concat_axis=2, tiled=True),
    )
    closing_cosine, closing_sine = angle_table(padded, padded, padded, 0, 0)
    value_entries = jnp.einsum(
        "xmj,jo->xmo", inverse_step_real, closing_cosine, precision=exact_setting
    ) - jnp.einsum("xmj,jo->xmo", inverse_step_imaginary, closing_sine, precision=exact_setting)
    return value_entries / period


def local(dense_coef, sparse_coef, pattern):
    block_count = dense_coef.shape[0]
    row_total = dense_coef.shape[2]
    spectra = forward(dense_coef)
    spec_shape = spectra[0].shape
    sparse = flatten(lax.all_gather(forward(sparse_coef), "blk", axis=1, tiled=True))
    empty_sum = jnp.zeros((block_count, spec_shape[1] * spec_shape[2]), jnp.float32)
    totals = (empty_sum, empty_sum)
    current = spectra
    for turn_index in range(STEPS + 1):
        if turn_index > 0:
            current = shifted(current, "blk", 1)
        totals = accumulate(totals, flatten(current), sparse, pattern, turn_index * block_count)
    value_entries = inverse(totals, spec_shape[1], spec_shape[2])
    lower_half = value_entries[:, :, :row_total]
    upper_half = value_entries[:, :, row_total:]
    carried_in = shifted(upper_half[-1:], "blk", 1)
    return lower_half + jnp.concatenate([carried_in, upper_half[:-1]], axis=0)


def solution(mesh):
    return jax.shard_map(
        local,
        mesh=mesh,
        in_specs=(
            P(("groups", "blk"), "sub", None),
            P(("groups", "blk"), "sub", None),
            P("groups"),
        ),
        out_specs=P(("groups", "blk"), "sub", None),
        check_vma=False,
    )
```

profile of v0, /device:TPU:0, one launch (start us, length us, event | category | flops | bytes accessed | tf_op | source)
XLA Modules:
  0.0 462.6 jit_solution(10227931367806987062)
XLA Ops:
  6.1 4.2 all-to-all-start.1
  14.5 7.6 %copy.18 = f32[2,32,32,256]{2,1,0,3:T(8,128)} copy(f32[2,32,32,256]{3,2,1,0:T(8,128)S(1)} %pad_maximum_fusion) | data formatting | bytes 4194304 | tf_op jit(solution)/shard_map/stack | solution.py:42
  22.1 7.1 %reshape.364 = f32[4,1,131072]{2,1,0:T(1,128)} reshape(f32[256,2,32,32]{3,2,1,0:T(8,128)} %bitcast.225) | data formatting | bytes 4194304
  29.2 4.5 all-to-all-start
  36.8 14.9 %all_gather.3 = f32[2,4,64,128]{3,2,1,0:T(8,128)S(1)} all-gather(f32[2,1,64,128]{3,2,1,0:T(8,128)S(1)} %pad_maximum_fusion.3), channel_id=1, replica_groups=mesh['groups'=2,'blk'=4,'sub'=4] {'blk'}, dimensions={1}, use_global_device_ids=true | all-gather | bytes 327680 | tf_op jit(solution)/shard_map/all_gather | solution.py:114
  52.0 7.4 %all-to-all-done = f32[4,1,131072]{2,1,0:T(1,128)} async-done(((f32[4,1,131072]{2,1,0:T(1,128)}), f32[4,1,131072]{2,1,0:T(1,128)}, u32[]{:S(2)}, u32[]{:S(2)}) %all-to-all-start) | async-done | bytes 2097184 | tf_op jit(solution)/shard_map/all_to_all | solution.py:44
  59.4 7.7 %reduce = f32[4,131072]{1,0:T(4,128)S(1)} reduce(f32[4,1,131072]{2,1,0:T(1,128)} %all-to-all-done, f32[]{:T(128)} %broadcast.711), dimensions={1}, to_apply=%all_to_all.48.reduce_sub_computation | reduce | bytes 4194308 | tf_op jit(solution)/shard_map/all_to_all | solution.py:44
  67.1 6.2 %reshape.365 = f32[256,2,32,32]{3,2,1,0:T(8,128)} reshape(f32[4,131072]{1,0:T(4,128)S(1)} %reduce) | data formatting | bytes 4194304
  73.3 8.1 %copy.19 = f32[2,32,32,4,64]{4,2,3,1,0:T(8,128)} copy(f32[2,32,32,4,64]{2,1,0,4,3:T(8,128)} %bitcast.226) | data formatting | bytes 4194304 | tf_op jit(solution)/shard_map/all_to_all | solution.py:44
  81.4 2.7 fusion.176
  84.1 3.5 fusion.59
  87.6 3.5 fusion.57
  91.1 3.5 convolution_add_fusion.1
  94.6 3.9 convolution_subtract_fusion.1
  103.3 36.4 %while.101 = (s32[]{:T(128)}, f32[32,8192]{1,0:T(8,128)S(1)}, f32[32,8192]{1,0:T(8,128)}, s32[4]{0:T(128)S(1)}, f32[32,8192]{1,0:T(8,128)S(1)}, /*index=5*/f32[4...) while((s32[]{:T(128)}, f32[32,8192]{1,0:T(8,128)S(1)}, ...), condition=%wide.region_1.3_spmd.clone, body=%wide.region_0.2_spmd.clone.sunk | while | flops 3671555 | bytes 10687239 | solution.py:77
  109.0 3.2 fusion.208
  117.9 3.5 fusion.208
  127.0 3.5 fusion.208
  136.2 3.5 fusion.208
  139.7 10.1 %collective-permute-done = f32[2,32,64,128]{3,2,1,0:T(8,128)} collective-permute-done((f32[2,32,64,128]{3,2,1,0:T(8,128)}, f32[2,32,64,128]{3,2,1,0:T(8,128)}, u32[]{:S(2)}, u32[]{:S(2)}) %collective-permute-start) | collective-permute-done | bytes 2097184 | tf_op jit(solution)/shard_map/ppermute | solution.py:14
  152.7 38.5 %while.96 = (s32[]{:T(128)}, f32[32,8192]{1,0:T(8,128)S(1)}, f32[32,8192]{1,0:T(8,128)}, s32[4]{0:T(128)S(1)}, f32[32,8192]{1,0:T(8,128)S(1)}, /*index=5*/f32[4,...) while((s32[]{:T(128)}, f32[32,8192]{1,0:T(8,128)S(1)}, ...), condition=%wide.region_3.5_spmd.clone, body=%wide.region_2.4_spmd.clone.sunk | while | flops 3147330 | bytes 10687221 | solution.py:77
  158.4 4.0 multiply_add_fusion.10
  168.0 4.0 multiply_add_fusion.10
  177.7 4.0 multiply_add_fusion.10
  187.3 4.0 multiply_add_fusion.10
  191.3 10.1 %collective-permute-done.1 = f32[2,32,64,128]{3,2,1,0:T(8,128)} collective-permute-done((f32[2,32,64,128]{3,2,1,0:T(8,128)}, f32[2,32,64,128]{3,2,1,0:T(8,128)}, u32[]{:S(2)}, u32[]{:S(2)}) %collective-permute-start.1) | collective-permute-done | bytes 2097184 | tf_op jit(solution)/shard_map/ppermute | solution.py:14
  204.3 38.7 %while.97 = (s32[]{:T(128)}, f32[32,8192]{1,0:T(8,128)S(1)}, f32[32,8192]{1,0:T(8,128)}, s32[4]{0:T(128)S(1)}, f32[32,8192]{1,0:T(8,128)S(1)}, /*index=5*/f32[4,...) while((s32[]{:T(128)}, f32[32,8192]{1,0:T(8,128)S(1)}, ...), condition=%wide.region_5.7_spmd.clone, body=%wide.region_4.6_spmd.clone.sunk | while | flops 3147330 | bytes 10687221 | solution.py:77
  210.1 4.0 multiply_add_fusion.11
  219.8 4.0 multiply_add_fusion.11
  229.4 4.0 multiply_add_fusion.11
  239.0 4.0 multiply_add_fusion.11
  243.0 9.0 %collective-permute-done.2 = f32[2,32,64,128]{3,2,1,0:T(8,128)} collective-permute-done((f32[2,32,64,128]{3,2,1,0:T(8,128)}, f32[2,32,64,128]{3,2,1,0:T(8,128)}, u32[]{:S(2)}, u32[]{:S(2)}) %collective-permute-start.2) | collective-permute-done | bytes 2097184 | tf_op jit(solution)/shard_map/ppermute | solution.py:14
  255.0 38.5 %while.98 = (s32[]{:T(128)}, f32[32,8192]{1,0:T(8,128)S(1)}, f32[32,8192]{1,0:T(8,128)}, s32[4]{0:T(128)S(1)}, f32[32,8192]{1,0:T(8,128)S(1)}, /*index=5*/f32[4,...) while((s32[]{:T(128)}, f32[32,8192]{1,0:T(8,128)S(1)}, ...), condition=%wide.region_7.9_spmd.clone, body=%wide.region_6.8_spmd.clone.sunk | while | flops 3147330 | bytes 10687221 | solution.py:77
  260.7 4.0 multiply_add_fusion.12
  270.3 4.0 multiply_add_fusion.12
  279.9 4.0 multiply_add_fusion.12
  289.5 4.0 multiply_add_fusion.12
  293.5 8.4 %collective-permute-done.3 = f32[2,32,64,128]{3,2,1,0:T(8,128)} collective-permute-done((f32[2,32,64,128]{3,2,1,0:T(8,128)}, f32[2,32,64,128]{3,2,1,0:T(8,128)}, u32[]{:S(2)}, u32[]{:S(2)}) %collective-permute-start.3) | collective-permute-done | bytes 2097184 | tf_op jit(solution)/shard_map/ppermute | solution.py:14
  304.8 38.5 %while.99 = (s32[]{:T(128)}, f32[32,8192]{1,0:T(8,128)S(1)}, f32[32,8192]{1,0:T(8,128)}, s32[4]{0:T(128)S(1)}, f32[32,8192]{1,0:T(8,128)S(1)}, /*index=5*/f32[4,...) while((s32[]{:T(128)}, f32[32,8192]{1,0:T(8,128)S(1)}, ...), condition=%wide.region_9.11_spmd.clone, body=%wide.region_8.10_spmd.clone.sunk | while | flops 3147330 | bytes 10687221 | solution.py:77
  310.5 4.0 multiply_add_fusion.13
  320.1 4.0 multiply_add_fusion.13
  329.8 4.0 multiply_add_fusion.13
  339.4 4.0 multiply_add_fusion.13
  343.3 7.5 %collective-permute-done.4 = f32[2,32,64,128]{3,2,1,0:T(8,128)} collective-permute-done((f32[2,32,64,128]{3,2,1,0:T(8,128)}, f32[2,32,64,128]{3,2,1,0:T(8,128)}, u32[]{:S(2)}, u32[]{:S(2)}) %collective-permute-start.4) | collective-permute-done | bytes 2097184 | tf_op jit(solution)/shard_map/ppermute | solution.py:14
  353.7 38.7 %while.100 = (s32[]{:T(128)}, f32[32,8192]{1,0:T(8,128)S(1)}, f32[32,8192]{1,0:T(8,128)}, s32[4]{0:T(128)S(1)}, f32[32,8192]{1,0:T(8,128)S(1)}, /*index=5*/f32[4...) while((s32[]{:T(128)}, f32[32,8192]{1,0:T(8,128)S(1)}, ...), condition=%wide.region_11.13_spmd.clone, body=%wide.region_10.12_spmd.clone.sunk | while | flops 3147330 | bytes 10687221 | solution.py:77
  359.4 4.0 multiply_add_fusion.14
  369.0 4.0 multiply_add_fusion.14
  378.7 4.0 multiply_add_fusion.14
  388.3 4.0 multiply_add_fusion.14
  396.6 2.8 add_bitcast_fusion
  399.4 3.1 copy.26
  402.5 2.4 reshape.368
  404.9 3.5 all-to-all-start.2
  408.4 3.1 copy.29
  413.9 8.9 %all-to-all-done.2 = f32[4,1,65536]{2,1,0:T(1,128)S(1)} async-done(((f32[4,1,65536]{2,1,0:T(1,128)}), f32[4,1,65536]{2,1,0:T(1,128)S(1)}, u32[]{:S(2)}, u32[]{:S(2)}) %all-to-all-start.2) | async-done | bytes 1048608 | tf_op jit(solution)/shard_map/all_to_all | solution.py:99
  423.8 4.7 %all-to-all-start.3 = ((f32[4,1,65536]{2,1,0:T(1,128)}), f32[4,1,65536]{2,1,0:T(1,128)}, u32[]{:S(2)}, u32[]{:S(2)}) async-start(f32[4,1,65536]{2,1,0:T(1,128)} %reshape.370), calls=%async_computation.3 | async-start | bytes 2097152 | tf_op jit(solution)/shard_map/all_to_all | solution.py:100
  428.5 4.6 %reduce.3 = f32[4,65536]{1,0:T(4,128)S(1)} reduce(f32[4,1,65536]{2,1,0:T(1,128)} %copy-done.4, f32[]{:T(128)} %broadcast.711), dimensions={1}, to_apply=%all_to_all.54.reduce_sub_computation | reduce | bytes 2097156 | tf_op jit(solution)/shard_map/all_to_all | solution.py:99
  434.1 2.7 copy.28
  436.8 2.6 all_to_all.57
  439.5 3.0 fusion.29
  443.0 4.6 %reduce.4 = f32[4,65536]{1,0:T(4,128)S(1)} reduce(f32[4,1,65536]{2,1,0:T(1,128)} %all-to-all-done.3, f32[]{:T(128)} %broadcast.711), dimensions={1}, to_apply=%all_to_all.58.reduce_sub_computation | reduce | bytes 2097156 | tf_op jit(solution)/shard_map/all_to_all | solution.py:100
  448.6 2.7 copy.31
  451.3 2.6 all_to_all.61
  456.0 5.5 %collective-permute-done.5 = f32[1,32,128]{2,1,0:T(8,128)S(1)} collective-permute-done((f32[1,32,128]{2,1,0:T(8,128)S(1)}, f32[1,32,128]{2,1,0:T(8,128)S(1)}, u32[]{:S(2)}, u32[]{:S(2)}) %collective-permute-start.5) | collective-permute-done | bytes 16416 | tf_op jit(solution)/shard_map/ppermute | solution.py:14
  (242 shorter events, 181.3 us)
Async XLA Ops:
  0.0 10.4 %copy-start = (f32[32,32,128]{2,1,0:T(8,128)S(1)}, f32[32,32,128]{2,1,0:T(8,128)}, u32[]{:S(2)}) copy-start(f32[32,32,128]{2,1,0:T(8,128)} %param.17) | copy-start | bytes 1572868
  6.1 23.0 %all-to-all-start.1 = ((f32[4,1,4096]{2,1,0:T(1,128)}), f32[4,1,4096]{2,1,0:T(1,128)S(1)}, u32[]{:S(2)}, u32[]{:S(2)}) async-start(f32[4,1,4096]{2,1,0:T(1,128)} %reshape.366), calls=%async_computation.1 | async-start | bytes 131072 | tf_op jit(solution)/shard_map/all_to_all | solution.py:44
  29.2 30.2 %all-to-all-start = ((f32[4,1,131072]{2,1,0:T(1,128)}), f32[4,1,131072]{2,1,0:T(1,128)}, u32[]{:S(2)}, u32[]{:S(2)}) async-start(f32[4,1,131072]{2,1,0:T(1,128)} %reshape.364), calls=%async_computation | async-start | bytes 4194304 | tf_op jit(solution)/shard_map/all_to_all | solution.py:44
  100.0 49.8 %collective-permute-start = (f32[2,32,64,128]{3,2,1,0:T(8,128)}, f32[2,32,64,128]{3,2,1,0:T(8,128)}, u32[]{:S(2)}, u32[]{:S(2)}) collective-permute-start(f32[2,32,64,128]{3,2,1,0:T(8,128)} %pad_maximum_fusion.1), channel_id=1, source_target_pairs={{12,0},{0,4},{4,8},{8,12},{13,1},{1,5},{5,9},{9,13},{14,2},{2,6},{... | collective-permute-start | bytes 6291464 | tf_op jit(solution)/shard_map/ppermute | solution.py:14
  102.1 1.2 copy-start.7
  152.7 48.7 %collective-permute-start.1 = (f32[2,32,64,128]{3,2,1,0:T(8,128)}, f32[2,32,64,128]{3,2,1,0:T(8,128)}, u32[]{:S(2)}, u32[]{:S(2)}) collective-permute-start(f32[2,32,64,128]{3,2,1,0:T(8,128)} %collective-permute-done), channel_id=1, source_target_pairs={{12,0},{0,4},{4,8},{8,12},{13,1},{1,5},{5,9},{9,13},{14,2},{2,6},{... | collective-permute-start | bytes 6291464 | tf_op jit(solution)/shard_map/ppermute | solution.py:14
  204.2 47.8 %collective-permute-start.2 = (f32[2,32,64,128]{3,2,1,0:T(8,128)}, f32[2,32,64,128]{3,2,1,0:T(8,128)}, u32[]{:S(2)}, u32[]{:S(2)}) collective-permute-start(f32[2,32,64,128]{3,2,1,0:T(8,128)} %collective-permute-done.1), channel_id=1, source_target_pairs={{12,0},{0,4},{4,8},{8,12},{13,1},{1,5},{5,9},{9,13},{14,2},{2,6},{... | collective-permute-start | bytes 6291464 | tf_op jit(solution)/shard_map/ppermute | solution.py:14
  254.9 47.0 %collective-permute-start.3 = (f32[2,32,64,128]{3,2,1,0:T(8,128)}, f32[2,32,64,128]{3,2,1,0:T(8,128)}, u32[]{:S(2)}, u32[]{:S(2)}) collective-permute-start(f32[2,32,64,128]{3,2,1,0:T(8,128)} %collective-permute-done.2), channel_id=1, source_target_pairs={{12,0},{0,4},{4,8},{8,12},{13,1},{1,5},{5,9},{9,13},{14,2},{2,6},{... | collective-permute-start | bytes 6291464 | tf_op jit(solution)/shard_map/ppermute | solution.py:14
  304.7 46.1 %collective-permute-start.4 = (f32[2,32,64,128]{3,2,1,0:T(8,128)}, f32[2,32,64,128]{3,2,1,0:T(8,128)}, u32[]{:S(2)}, u32[]{:S(2)}) collective-permute-start(f32[2,32,64,128]{3,2,1,0:T(8,128)} %collective-permute-done.3), channel_id=1, source_target_pairs={{12,0},{0,4},{4,8},{8,12},{13,1},{1,5},{5,9},{9,13},{14,2},{2,6},{... | collective-permute-start | bytes 6291464 | tf_op jit(solution)/shard_map/ppermute | solution.py:14
  392.6 2.5 copy-start.2
  395.4 1.3 copy-start.5
  395.4 1.3 copy-start.6
  404.9 17.9 %all-to-all-start.2 = ((f32[4,1,65536]{2,1,0:T(1,128)}), f32[4,1,65536]{2,1,0:T(1,128)S(1)}, u32[]{:S(2)}, u32[]{:S(2)}) async-start(f32[4,1,65536]{2,1,0:T(1,128)} %reshape.368), calls=%async_computation.2 | async-start | bytes 2097152 | tf_op jit(solution)/shard_map/all_to_all | solution.py:99
  422.8 1.0 copy-start.4
  423.8 19.1 %all-to-all-start.3 = ((f32[4,1,65536]{2,1,0:T(1,128)}), f32[4,1,65536]{2,1,0:T(1,128)}, u32[]{:S(2)}, u32[]{:S(2)}) async-start(f32[4,1,65536]{2,1,0:T(1,128)} %reshape.370), calls=%async_computation.3 | async-start | bytes 2097152 | tf_op jit(solution)/shard_map/all_to_all | solution.py:100
  451.3 2.6 copy-start.3
  451.3 11.1 %copy-start.1 = (f32[32,32,128]{2,1,0:T(8,128)S(1)}, f32[32,32,128]{2,1,0:T(8,128)}, u32[]{:S(2)}) copy-start(f32[32,32,128]{2,1,0:T(8,128)} %param.17) | copy-start | bytes 1572868
  455.9 5.6 %collective-permute-start.5 = (f32[1,32,128]{2,1,0:T(8,128)S(1)}, f32[1,32,128]{2,1,0:T(8,128)S(1)}, u32[]{:S(2)}, u32[]{:S(2)}) collective-permute-start(f32[1,32,128]{2,1,0:T(8,128)S(1)} %slice.124), channel_id=1, source_target_pairs={{12,0},{0,4},{4,8},{8,12},{13,1},{1,5},{5,9},{9,13},{14,2},{2,6},{... | collective-permute-start | bytes 49160 | tf_op jit(solution)/shard_map/ppermute | solution.py:14
where the time goes:
time: 472 us; the launch traced here: 463 us
  local copies, waits for them, and re-layouts  179 us (38%)
  other arithmetic  147 us (31%)
  waiting for transfers between devices  67.4 us (14%)
  matrix products  33.5 us (7%)
  starting transfers between devices  19.3 us (4%)
  blocking collectives  14.9 us (3%)
    add x24, other arithmetic, one_entry(): running[1] + src_real * sp_imag + src_imag * sp_real  92.9 us
    ppermute x6, waiting for transfers between devices, shifted(): return lax.ppermute(block, axis, route)  50.6 us
    gather x24, local copies, waits for them, and re-layouts, one_entry(): src_real = jnp.where(valid, jnp.take(source[0], safe, axis=0), 0.0)  44.2 us
    gather x24, local copies, waits for them, and re-layouts, one_entry(): src_imag = jnp.where(valid, jnp.take(source[1], safe, axis=0), 0.0)  44 us
    unnamed x27, local copies, waits for them, and re-layouts  22.9 us
    and x24, other arithmetic, one_entry(): src_real = jnp.where(valid, jnp.take(source[0], safe, axis=0), 0.0)  15.8 us
    select_n x24, other arithmetic, one_entry(): src_real = jnp.where(valid, jnp.take(source[0], safe, axis=0), 0.0)  15.6 us
    all_gather x1, blocking collectives, local(): lax.all_gather(forward(sparse_coef), 'blk', axis=1, tiled=True)  14.9 us
  transfers between devices with their start and end apart: 10, of which 9 were waited for; matrix products, arithmetic and copies ran while one was open for 50% of the time, Pallas kernels for 0%

commit v1 on v0

--- a/solution.py
+++ b/solution.py
@@ -41,7 +41,9 @@
     turned_imag = initial_imaginary * twist_cos - initial_real * twist_sin
     stacked = jnp.stack([turned_real, turned_imag], axis=0)
     outer_cosine, outer_sine = angle_table(col_total, col_total, col_total, 0, 0)
-    halves = lax.all_to_all(stacked, "sub", split_axis=3, concat_axis=2, tiled=True)
+    pieces = jnp.split(stacked, lax.axis_size("sub"), axis=3)
+    incoming = lax.all_to_all(jnp.stack(pieces), "sub", 0, 0)
+    halves = jnp.concatenate(incoming, axis=2)
     partial_real = halves[0]
     partial_imaginary = halves[1]
     output_real = jnp.einsum(

time: 472 us -> 451 us (0.956)
  local copies, waits for them, and re-layouts: 179 us -> 158 us
    all_to_all x3 -> x1, local copies, waits for them, and re-layouts: 8.79 us -> 0.51 us  [forward(): incoming = lax.all_to_all(jnp.stack(pieces), 'sub', 0, 0)]
    another operation x2 -> x1, local copies, waits for them, and re-layouts: 7.74 us -> 0.08 us  [forward(): incoming = lax.all_to_all(jnp.stack(pieces), 'sub', 0, 0)]
where the time goes in v1:
time: 451 us; the launch traced here: 443 us
  local copies, waits for them, and re-layouts  158 us (35%)
  other arithmetic  147 us (33%)
  waiting for transfers between devices  68.8 us (15%)
  matrix products  32.8 us (7%)
  starting transfers between devices  19.6 us (4%)
  blocking collectives  15.2 us (3%)
    add x24, other arithmetic, one_entry(): running[1] + src_real * sp_imag + src_imag * sp_real  92.4 us
    ppermute x6, waiting for transfers between devices, shifted(): return lax.ppermute(block, axis, route)  52.3 us
    gather x24, local copies, waits for them, and re-layouts, one_entry(): src_real = jnp.where(valid, jnp.take(source[0], safe, axis=0), 0.0)  44 us
    gather x24, local copies, waits for them, and re-layouts, one_entry(): src_imag = jnp.where(valid, jnp.take(source[1], safe, axis=0), 0.0)  43.8 us
    unnamed x27, local copies, waits for them, and re-layouts  18.6 us
    all_gather x1, blocking collectives, local(): lax.all_gather(forward(sparse_coef), 'blk', axis=1, tiled=True)  15.2 us
    and x24, other arithmetic, one_entry(): src_real = jnp.where(valid, jnp.take(source[0], safe, axis=0), 0.0)  15 us
    select_n x24, other arithmetic, one_entry(): src_real = jnp.where(valid, jnp.take(source[0], safe, axis=0), 0.0)  14.9 us
  transfers between devices with their start and end apart: 10, of which 9 were waited for; matrix products, arithmetic and copies ran while one was open for 50% of the time, Pallas kernels for 0%

profile of v1, /device:TPU:0, one launch (start us, length us, event | category | flops | bytes accessed | tf_op | source)
XLA Modules:
  0.0 443.3 jit_solution(7484291468514546414)
XLA Ops:
  3.9 4.2 all-to-all-start.1
  12.8 2.8 pad_maximum_fusion
  15.6 5.5 %reshape.374 = f32[4,1,131072]{2,1,0:T(1,128)} reshape(f32[4,2,32,32,64]{4,3,2,1,0:T(8,128)} %pad_maximum_fusion) | data formatting | bytes 4194304
  21.1 4.4 %all-to-all-start = ((f32[4,1,131072]{2,1,0:T(1,128)}), f32[4,1,131072]{2,1,0:T(1,128)}, u32[]{:S(2)}, u32[]{:S(2)}) async-start(f32[4,1,131072]{2,1,0:T(1,128)} %reshape.374), calls=%async_computation | async-start | bytes 4194304 | tf_op jit(solution)/shard_map/all_to_all | solution.py:45
  28.9 15.2 %all_gather.3 = f32[2,4,64,128]{3,2,1,0:T(8,128)S(1)} all-gather(f32[2,1,64,128]{3,2,1,0:T(8,128)S(1)} %pad_maximum_fusion.5), channel_id=1, replica_groups=mesh['groups'=2,'blk'=4,'sub'=4] {'blk'}, dimensions={1}, use_global_device_ids=true | all-gather | bytes 327680 | tf_op jit(solution)/shard_map/all_gather | solution.py:116
  44.3 7.0 %all-to-all-done = f32[4,1,131072]{2,1,0:T(1,128)} async-done(((f32[4,1,131072]{2,1,0:T(1,128)}), f32[4,1,131072]{2,1,0:T(1,128)}, u32[]{:S(2)}, u32[]{:S(2)}) %all-to-all-start) | async-done | bytes 2097184 | tf_op jit(solution)/shard_map/all_to_all | solution.py:45
  51.3 7.7 %reduce = f32[4,131072]{1,0:T(4,128)S(1)} reduce(f32[4,1,131072]{2,1,0:T(1,128)} %all-to-all-done, f32[]{:T(128)} %broadcast.711), dimensions={1}, to_apply=%all_to_all.32.reduce_sub_computation | reduce | bytes 4194308 | tf_op jit(solution)/shard_map/all_to_all | solution.py:45
  59.0 4.0 reshape.375
  63.0 3.0 fusion.186
  66.2 3.5 fusion.65
  69.9 3.6 fusion.67
  73.6 3.5 convolution_subtract_fusion.1
  77.1 3.5 convolution_add_fusion.1
  82.0 2.3 collective-permute-start
  85.6 35.7 %while.101 = (s32[]{:T(128)}, f32[32,8192]{1,0:T(8,128)S(1)}, f32[32,8192]{1,0:T(8,128)}, s32[4]{0:T(128)S(1)}, f32[32,8192]{1,0:T(8,128)S(1)}, /*index=5*/f32[4...) while((s32[]{:T(128)}, f32[32,8192]{1,0:T(8,128)S(1)}, ...), condition=%wide.region_1.3_spmd.clone, body=%wide.region_0.2_spmd.clone.sunk | while | flops 3671555 | bytes 10687247 | solution.py:79
  91.1 3.2 fusion.219
  99.8 3.5 fusion.219
  108.8 3.5 fusion.219
  117.7 3.5 fusion.219
  121.2 10.8 %collective-permute-done = f32[2,32,64,128]{3,2,1,0:T(8,128)} collective-permute-done((f32[2,32,64,128]{3,2,1,0:T(8,128)}, f32[2,32,64,128]{3,2,1,0:T(8,128)}, u32[]{:S(2)}, u32[]{:S(2)}) %collective-permute-start) | collective-permute-done | bytes 2097184 | tf_op jit(solution)/shard_map/ppermute | solution.py:14
  135.0 38.3 %while.96 = (s32[]{:T(128)}, f32[32,8192]{1,0:T(8,128)S(1)}, f32[32,8192]{1,0:T(8,128)}, s32[4]{0:T(128)S(1)}, f32[32,8192]{1,0:T(8,128)S(1)}, /*index=5*/f32[4,...) while((s32[]{:T(128)}, f32[32,8192]{1,0:T(8,128)S(1)}, ...), condition=%wide.region_3.5_spmd.clone, body=%wide.region_2.4_spmd.clone.sunk | while | flops 3147330 | bytes 10687229 | solution.py:79
  140.6 3.9 multiply_add_fusion.10
  150.2 3.9 multiply_add_fusion.10
  159.7 3.9 multiply_add_fusion.10
  169.3 3.9 multiply_add_fusion.10
  173.2 10.3 %collective-permute-done.1 = f32[2,32,64,128]{3,2,1,0:T(8,128)} collective-permute-done((f32[2,32,64,128]{3,2,1,0:T(8,128)}, f32[2,32,64,128]{3,2,1,0:T(8,128)}, u32[]{:S(2)}, u32[]{:S(2)}) %collective-permute-start.1) | collective-permute-done | bytes 2097184 | tf_op jit(solution)/shard_map/ppermute | solution.py:14
  186.5 37.6 %while.97 = (s32[]{:T(128)}, f32[32,8192]{1,0:T(8,128)S(1)}, f32[32,8192]{1,0:T(8,128)}, s32[4]{0:T(128)S(1)}, f32[32,8192]{1,0:T(8,128)S(1)}, /*index=5*/f32[4,...) while((s32[]{:T(128)}, f32[32,8192]{1,0:T(8,128)S(1)}, ...), condition=%wide.region_5.7_spmd.clone, body=%wide.region_4.6_spmd.clone.sunk | while | flops 3147330 | bytes 10687229 | solution.py:79
  192.0 3.9 multiply_add_fusion.11
  201.4 3.9 multiply_add_fusion.11
  210.8 3.9 multiply_add_fusion.11
  220.2 3.9 multiply_add_fusion.11
  224.2 10.1 %collective-permute-done.2 = f32[2,32,64,128]{3,2,1,0:T(8,128)} collective-permute-done((f32[2,32,64,128]{3,2,1,0:T(8,128)}, f32[2,32,64,128]{3,2,1,0:T(8,128)}, u32[]{:S(2)}, u32[]{:S(2)}) %collective-permute-start.2) | collective-permute-done | bytes 2097184 | tf_op jit(solution)/shard_map/ppermute | solution.py:14
  237.6 38.4 %while.98 = (s32[]{:T(128)}, f32[32,8192]{1,0:T(8,128)S(1)}, f32[32,8192]{1,0:T(8,128)}, s32[4]{0:T(128)S(1)}, f32[32,8192]{1,0:T(8,128)S(1)}, /*index=5*/f32[4,...) while((s32[]{:T(128)}, f32[32,8192]{1,0:T(8,128)S(1)}, ...), condition=%wide.region_7.9_spmd.clone, body=%wide.region_6.8_spmd.clone.sunk | while | flops 3147330 | bytes 10687229 | solution.py:79
  243.3 3.9 multiply_add_fusion.12
  252.9 3.9 multiply_add_fusion.12
  262.5 3.9 multiply_add_fusion.12
  272.1 3.9 multiply_add_fusion.12
  276.0 8.5 %collective-permute-done.3 = f32[2,32,64,128]{3,2,1,0:T(8,128)} collective-permute-done((f32[2,32,64,128]{3,2,1,0:T(8,128)}, f32[2,32,64,128]{3,2,1,0:T(8,128)}, u32[]{:S(2)}, u32[]{:S(2)}) %collective-permute-start.3) | collective-permute-done | bytes 2097184 | tf_op jit(solution)/shard_map/ppermute | solution.py:14
  287.5 38.9 %while.99 = (s32[]{:T(128)}, f32[32,8192]{1,0:T(8,128)S(1)}, f32[32,8192]{1,0:T(8,128)}, s32[4]{0:T(128)S(1)}, f32[32,8192]{1,0:T(8,128)S(1)}, /*index=5*/f32[4,...) while((s32[]{:T(128)}, f32[32,8192]{1,0:T(8,128)S(1)}, ...), condition=%wide.region_9.11_spmd.clone, body=%wide.region_8.10_spmd.clone.sunk | while | flops 3147330 | bytes 10687229 | solution.py:79
  293.3 3.9 multiply_add_fusion.13
  303.0 3.9 multiply_add_fusion.13
  312.7 3.9 multiply_add_fusion.13
  322.4 3.9 multiply_add_fusion.13
  326.3 7.1 %collective-permute-done.4 = f32[2,32,64,128]{3,2,1,0:T(8,128)} collective-permute-done((f32[2,32,64,128]{3,2,1,0:T(8,128)}, f32[2,32,64,128]{3,2,1,0:T(8,128)}, u32[]{:S(2)}, u32[]{:S(2)}) %collective-permute-start.4) | collective-permute-done | bytes 2097184 | tf_op jit(solution)/shard_map/ppermute | solution.py:14
  336.4 38.6 %while.100 = (s32[]{:T(128)}, f32[32,8192]{1,0:T(8,128)S(1)}, f32[32,8192]{1,0:T(8,128)}, s32[4]{0:T(128)S(1)}, f32[32,8192]{1,0:T(8,128)S(1)}, /*index=5*/f32[4...) while((s32[]{:T(128)}, f32[32,8192]{1,0:T(8,128)S(1)}, ...), condition=%wide.region_11.13_spmd.clone, body=%wide.region_10.12_spmd.clone.sunk | while | flops 3147330 | bytes 10687229 | solution.py:79
  342.0 3.9 multiply_add_fusion.14
  351.6 3.9 multiply_add_fusion.14
  361.2 3.9 multiply_add_fusion.14
  370.8 3.9 multiply_add_fusion.14
  379.2 2.4 add_bitcast_fusion
  383.4 2.4 reshape.378
  385.8 3.5 all-to-all-start.2
  389.3 3.1 copy.34
  392.4 2.4 reshape.380
  394.8 8.9 %all-to-all-done.2 = f32[4,1,65536]{2,1,0:T(1,128)S(1)} async-done(((f32[4,1,65536]{2,1,0:T(1,128)}), f32[4,1,65536]{2,1,0:T(1,128)S(1)}, u32[]{:S(2)}, u32[]{:S(2)}) %all-to-all-start.2) | async-done | bytes 1048608 | tf_op jit(solution)/shard_map/all_to_all | solution.py:101
  404.7 4.4 %all-to-all-start.3 = ((f32[4,1,65536]{2,1,0:T(1,128)}), f32[4,1,65536]{2,1,0:T(1,128)}, u32[]{:S(2)}, u32[]{:S(2)}) async-start(f32[4,1,65536]{2,1,0:T(1,128)} %reshape.380), calls=%async_computation.3 | async-start | bytes 2097152 | tf_op jit(solution)/shard_map/all_to_all | solution.py:102
  409.1 4.6 %reduce.2 = f32[4,65536]{1,0:T(4,128)S(1)} reduce(f32[4,1,65536]{2,1,0:T(1,128)} %copy-done.4, f32[]{:T(128)} %broadcast.711), dimensions={1}, to_apply=%all_to_all.34.reduce_sub_computation | reduce | bytes 2097156 | tf_op jit(solution)/shard_map/all_to_all | solution.py:101
  414.8 2.7 copy.33
  417.5 2.7 all_to_all.37
  420.2 2.9 fusion.36
  423.6 4.6 %reduce.3 = f32[4,65536]{1,0:T(4,128)S(1)} reduce(f32[4,1,65536]{2,1,0:T(1,128)} %all-to-all-done.3, f32[]{:T(128)} %broadcast.711), dimensions={1}, to_apply=%all_to_all.38.reduce_sub_computation | reduce | bytes 2097156 | tf_op jit(solution)/shard_map/all_to_all | solution.py:102
  429.2 2.7 copy.36
  431.9 2.6 all_to_all.41
  436.7 5.5 %collective-permute-done.5 = f32[1,32,128]{2,1,0:T(8,128)S(1)} collective-permute-done((f32[1,32,128]{2,1,0:T(8,128)S(1)}, f32[1,32,128]{2,1,0:T(8,128)S(1)}, u32[]{:S(2)}, u32[]{:S(2)}) %collective-permute-start.5) | collective-permute-done | bytes 16416 | tf_op jit(solution)/shard_map/ppermute | solution.py:14
  (244 shorter events, 176.6 us)
Async XLA Ops:
  0.0 8.1 %copy-start = (f32[32,32,128]{2,1,0:T(8,128)S(1)}, f32[32,32,128]{2,1,0:T(8,128)}, u32[]{:S(2)}) copy-start(f32[32,32,128]{2,1,0:T(8,128)} %param.17) | copy-start | bytes 1572868
  3.9 17.3 %all-to-all-start.1 = ((f32[4,1,4096]{2,1,0:T(1,128)}), f32[4,1,4096]{2,1,0:T(1,128)S(1)}, u32[]{:S(2)}, u32[]{:S(2)}) async-start(f32[4,1,4096]{2,1,0:T(1,128)} %reshape.376), calls=%async_computation.1 | async-start | bytes 131072 | tf_op jit(solution)/shard_map/all_to_all | solution.py:45
  21.1 30.2 %all-to-all-start = ((f32[4,1,131072]{2,1,0:T(1,128)}), f32[4,1,131072]{2,1,0:T(1,128)}, u32[]{:S(2)}, u32[]{:S(2)}) async-start(f32[4,1,131072]{2,1,0:T(1,128)} %reshape.374), calls=%async_computation | async-start | bytes 4194304 | tf_op jit(solution)/shard_map/all_to_all | solution.py:45
  82.0 50.0 %collective-permute-start = (f32[2,32,64,128]{3,2,1,0:T(8,128)}, f32[2,32,64,128]{3,2,1,0:T(8,128)}, u32[]{:S(2)}, u32[]{:S(2)}) collective-permute-start(f32[2,32,64,128]{3,2,1,0:T(8,128)} %pad_maximum_fusion.1), channel_id=1, source_target_pairs={{12,0},{0,4},{4,8},{8,12},{13,1},{1,5},{5,9},{9,13},{14,2},{2,6},{... | collective-permute-start | bytes 6291464 | tf_op jit(solution)/shard_map/ppermute | solution.py:14
  84.4 1.2 copy-start.7
  134.9 48.7 %collective-permute-start.1 = (f32[2,32,64,128]{3,2,1,0:T(8,128)}, f32[2,32,64,128]{3,2,1,0:T(8,128)}, u32[]{:S(2)}, u32[]{:S(2)}) collective-permute-start(f32[2,32,64,128]{3,2,1,0:T(8,128)} %collective-permute-done), channel_id=1, source_target_pairs={{12,0},{0,4},{4,8},{8,12},{13,1},{1,5},{5,9},{9,13},{14,2},{2,6},{... | collective-permute-start | bytes 6291464 | tf_op jit(solution)/shard_map/ppermute | solution.py:14
  186.5 47.8 %collective-permute-start.2 = (f32[2,32,64,128]{3,2,1,0:T(8,128)}, f32[2,32,64,128]{3,2,1,0:T(8,128)}, u32[]{:S(2)}, u32[]{:S(2)}) collective-permute-start(f32[2,32,64,128]{3,2,1,0:T(8,128)} %collective-permute-done.1), channel_id=1, source_target_pairs={{12,0},{0,4},{4,8},{8,12},{13,1},{1,5},{5,9},{9,13},{14,2},{2,6},{... | collective-permute-start | bytes 6291464 | tf_op jit(solution)/shard_map/ppermute | solution.py:14
  237.1 47.4 %collective-permute-start.3 = (f32[2,32,64,128]{3,2,1,0:T(8,128)}, f32[2,32,64,128]{3,2,1,0:T(8,128)}, u32[]{:S(2)}, u32[]{:S(2)}) collective-permute-start(f32[2,32,64,128]{3,2,1,0:T(8,128)} %collective-permute-done.2), channel_id=1, source_target_pairs={{12,0},{0,4},{4,8},{8,12},{13,1},{1,5},{5,9},{9,13},{14,2},{2,6},{... | collective-permute-start | bytes 6291464 | tf_op jit(solution)/shard_map/ppermute | solution.py:14
  287.4 46.1 %collective-permute-start.4 = (f32[2,32,64,128]{3,2,1,0:T(8,128)}, f32[2,32,64,128]{3,2,1,0:T(8,128)}, u32[]{:S(2)}, u32[]{:S(2)}) collective-permute-start(f32[2,32,64,128]{3,2,1,0:T(8,128)} %collective-permute-done.3), channel_id=1, source_target_pairs={{12,0},{0,4},{4,8},{8,12},{13,1},{1,5},{5,9},{9,13},{14,2},{2,6},{... | collective-permute-start | bytes 6291464 | tf_op jit(solution)/shard_map/ppermute | solution.py:14
  375.1 2.5 copy-start.2
  377.8 1.3 copy-start.5
  377.9 1.3 copy-start.6
  385.8 17.9 %all-to-all-start.2 = ((f32[4,1,65536]{2,1,0:T(1,128)}), f32[4,1,65536]{2,1,0:T(1,128)S(1)}, u32[]{:S(2)}, u32[]{:S(2)}) async-start(f32[4,1,65536]{2,1,0:T(1,128)} %reshape.378), calls=%async_computation.2 | async-start | bytes 2097152 | tf_op jit(solution)/shard_map/all_to_all | solution.py:101
  403.7 1.0 copy-start.4
  404.7 18.9 %all-to-all-start.3 = ((f32[4,1,65536]{2,1,0:T(1,128)}), f32[4,1,65536]{2,1,0:T(1,128)}, u32[]{:S(2)}, u32[]{:S(2)}) async-start(f32[4,1,65536]{2,1,0:T(1,128)} %reshape.380), calls=%async_computation.3 | async-start | bytes 2097152 | tf_op jit(solution)/shard_map/all_to_all | solution.py:102
  431.9 2.6 copy-start.3
  431.9 11.1 %copy-start.1 = (f32[32,32,128]{2,1,0:T(8,128)S(1)}, f32[32,32,128]{2,1,0:T(8,128)}, u32[]{:S(2)}) copy-start(f32[32,32,128]{2,1,0:T(8,128)} %param.17) | copy-start | bytes 1572868
  436.5 5.6 %collective-permute-start.5 = (f32[1,32,128]{2,1,0:T(8,128)S(1)}, f32[1,32,128]{2,1,0:T(8,128)S(1)}, u32[]{:S(2)}, u32[]{:S(2)}) collective-permute-start(f32[1,32,128]{2,1,0:T(8,128)S(1)} %slice.124), channel_id=1, source_target_pairs={{12,0},{0,4},{4,8},{8,12},{13,1},{1,5},{5,9},{9,13},{14,2},{2,6},{... | collective-permute-start | bytes 49160 | tf_op jit(solution)/shard_map/ppermute | solution.py:14
